TPU v7x, 128 devices: a whole 4x4x4 slice. The times are simulated.
128 devices in a mesh: dp: 16 (over x, y), tensor: 8 (over z, core).
Axes of the slice: x: 4, y: 4, z: 4, core: 2. Of those that a mesh axis runs over, the one named last changes fastest.
Arguments:
- tokens: bfloat16 [256, 5376], P('dp'), may hold values from -6 to 6
- lengths: int32 [256], P('dp'), may hold values from 1 to 1024, as said below
- positions: int32 [256], P('dp'), may hold values from 1 to 33791, as said below
- in_gain: float32 [5376], replicated, may hold values from 0.25 to 1.75
- q_weight: bfloat16 [5376, 4096], P('dp', 'tensor'), may hold values from -0.078125 to 0.078125
- k_weight: bfloat16 [5376, 2048], P('dp', 'tensor'), may hold values from -0.078125 to 0.078125
- v_weight: bfloat16 [5376, 2048], P('dp', 'tensor'), may hold values from -0.078125 to 0.078125
- q_gain: float32 [128], replicated, may hold values from 0.1 to 1.9
- k_gain: float32 [128], replicated, may hold values from 0.1 to 1.9
- key_cache: bfloat16 [256, 1024, 2048], P('dp', None, 'tensor'), may hold values from -480 to 480
- value_cache: bfloat16 [256, 1024, 2048], P('dp', None, 'tensor'), may hold values from -6 to 6
- out_weight: bfloat16 [4096, 5376], P('tensor', 'dp'), may hold values from -0.09375 to 0.09375
- post_gain: float32 [5376], replicated, may hold values from 0.25 to 1.75
Outputs:
- hidden_out: bfloat16 [256, 5376], P('dp')
- new_keys: bfloat16 [256, 2048], P('dp', 'tensor')
- new_values: bfloat16 [256, 2048], P('dp', 'tensor')
Inputs may be any that keep to these rules, and one draw needn't show every extreme that they name: Slots 0 to lengths - 1 of a sequence hold its cache; some sequence has exactly 1024. `positions`: each position is at least the sequence's length.
All inputs are finite; a program needn't handle non-finite values.
Results may differ from a plain program's by a relative error of at most 0.012.
The roundings to bfloat16 on the way count: a program that leaves them out, or rounds other values in their place, can miss the bound.
Values may be sent and summed in bfloat16 or wider, within the bound.
A program may use at most 64 MiB of HBM per device.

v0:
```python
import jax
import jax.numpy as jnp
from jax import lax
from jax.sharding import PartitionSpec as P

HD = 128
QPRE = 168


epsilon = 1e-06
rope_base = 1000000.0
rope_factor = 8.0


def cut_along(array, dim, peers):
    before, after = (array.shape[:dim], array.shape[dim + 1 :])
    return jnp.moveaxis(array.reshape(*before, peers, -1, *after), dim, 0)


def summed_on_arrival(array, axis, dim):
    peers = lax.axis_size(axis)
    pieces = lax.all_to_all(cut_along(array, dim, peers), axis, 0, 0, tiled=True)
    return jnp.sum(pieces, axis=0)


def copy_for_each(array, axis):
    peers = lax.axis_size(axis)
    return lax.all_to_all(
        jnp.broadcast_to(array[None], (peers, *array.shape)), axis, 0, 0, tiled=True
    )


def joined_along(pieces, dim):
    shape = list(pieces.shape[1:])
    shape[dim] *= pieces.shape[0]
    return jnp.moveaxis(pieces, 0, dim).reshape(shape)


def collect(array, axis, dim):
    pieces = copy_for_each(array, axis)
    return joined_along(pieces, dim)


def gathered_total(array, axis):
    return lax.all_gather(array, axis).sum(0)


def rms_scale(vectors, gain):
    mean_square = jnp.mean(vectors * vectors, axis=-1, keepdims=True)
    return vectors * lax.rsqrt(mean_square + epsilon) * gain


def rotate(vectors, positions):
    half_width = vectors.shape[-1] // 2
    exponent = jnp.arange(half_width, dtype=jnp.float32) * (2.0 / vectors.shape[-1])
    frequency = jnp.power(rope_base, -exponent)
    angles = (positions.astype(jnp.float32) / rope_factor)[:, None] * frequency[None, :]
    cos_part = jnp.cos(angles)[:, None, :]
    sin_part = jnp.sin(angles)[:, None, :]
    first_half = vectors[..., :half_width]
    second_half = vectors[..., half_width:]
    return jnp.concatenate(
        [
            first_half * cos_part - second_half * sin_part,
            second_half * cos_part + first_half * sin_part,
        ],
        axis=-1,
    )


def per_device(
    tokens,
    lengths,
    positions,
    in_gain,
    q_weight,
    k_weight,
    v_weight,
    q_gain,
    k_gain,
    key_cache,
    value_cache,
    out_weight,
    post_gain,
):
    tok_rows = tokens.shape[0]
    q_cols = q_weight.shape[1]
    kv_cols = k_weight.shape[1]
    local_heads = q_cols // HD
    local_kv = kv_cols // HD
    per_group = local_heads // local_kv
    cache_len = key_cache.shape[1]
    normed = rms_scale(tokens.astype(jnp.float32), in_gain).astype(jnp.bfloat16)
    spread = lax.all_to_all(normed, "dp", split_axis=1, concat_axis=0, tiled=True)
    joined = summed_on_arrival(
        jnp.concatenate(
            [
                jnp.dot(spread, q_weight, preferred_element_type=jnp.float32),
                jnp.dot(spread, k_weight, preferred_element_type=jnp.float32),
                jnp.dot(spread, v_weight, preferred_element_type=jnp.float32),
            ],
            axis=1,
        ),
        "dp",
        0,
    )
    q_raw = joined[:, :q_cols]
    k_raw = joined[:, q_cols : q_cols + kv_cols]
    v_raw = joined[:, q_cols + kv_cols :]
    new_values = v_raw.astype(jnp.bfloat16)
    queries = (
        rotate(rms_scale(q_raw.reshape(tok_rows, local_heads, HD), q_gain), positions)
        * QPRE ** (-0.5)
    ).astype(jnp.bfloat16)
    new_keys = (
        rotate(rms_scale(k_raw.reshape(tok_rows, local_kv, HD), k_gain), positions)
        .astype(jnp.bfloat16)
        .reshape(tok_rows, kv_cols)
    )
    grouped = queries.reshape(tok_rows, local_kv, per_group, HD)
    cache_keys = key_cache.reshape(tok_rows, cache_len, local_kv, HD)
    cache_values = value_cache.reshape(tok_rows, cache_len, local_kv, HD)
    self_score = jnp.einsum(
        "bgrd,bgd->bgr",
        grouped,
        new_keys.reshape(tok_rows, local_kv, HD),
        preferred_element_type=jnp.float32,
    )
    self_values = new_values.reshape(tok_rows, local_kv, HD).astype(jnp.float32)
    scores = jnp.einsum("bgrd,bjgd->bgrj", grouped, cache_keys, preferred_element_type=jnp.float32)
    usable = jnp.arange(cache_len)[None, :] < lengths[:, None]
    scores = jnp.where(usable[:, None, None, :], scores, -jnp.inf)
    largest = jnp.maximum(jnp.max(scores, axis=-1), self_score)
    weights = jnp.exp(scores - largest[..., None])
    self_weight = jnp.exp(self_score - largest)
    running = jnp.sum(weights, axis=-1) + self_weight
    rounded_self = lax.optimization_barrier(self_weight.astype(jnp.bfloat16)).astype(jnp.float32)
    mixture = jnp.einsum(
        "bgrj,bjgd->bgrd",
        weights.astype(jnp.bfloat16),
        cache_values,
        preferred_element_type=jnp.float32,
    )
    mixture = mixture + rounded_self[..., None] * self_values[:, :, None, :]
    attended = (mixture / running[..., None]).reshape(tok_rows, q_cols).astype(jnp.bfloat16)
    products = jnp.dot(collect(attended, "dp", 0), out_weight, preferred_element_type=jnp.float32)
    partial_value = lax.all_to_all(products, "dp", split_axis=0, concat_axis=1, tiled=True)
    summed = gathered_total(partial_value, "tensor")
    hidden_out = (tokens.astype(jnp.float32) + rms_scale(summed, post_gain)).astype(jnp.bfloat16)
    return (hidden_out, new_keys, new_values)


def solution(mesh):
    return jax.shard_map(
        per_device,
        mesh=mesh,
        in_specs=(
            P("dp", None),
            P("dp"),
            P("dp"),
            P(),
            P("dp", "tensor"),
            P("dp", "tensor"),
            P("dp", "tensor"),
            P(),
            P(),
            P("dp", None, "tensor"),
            P("dp", None, "tensor"),
            P("tensor", "dp"),
            P(),
        ),
        out_specs=(P("dp", None), P("dp", "tensor"), P("dp", "tensor")),
        check_vma=False,
    )
```

profile of v0, /device:TPU:1, one launch (start us, length us, event | category | flops | bytes accessed | tf_op | source)
XLA Modules:
  0.0 122.7 jit_solution(7324645535580208920)
XLA Ops:
  7.2 0.0 copy-start
  7.2 0.0 copy-start.6
  7.2 0.0 copy-start.5
  7.2 1.1 fusion.18
  8.3 1.0 fusion.20
  9.4 0.3 all_to_all.30
  9.7 14.5 %all_to_all.42 = bf16[16,16,336]{2,0,1:T(8,128)(2,1)S(1)} all-to-all(bf16[16,16,336]{2,0,1:T(8,128)(2,1)S(1)} %copy.26), channel_id=1, replica_groups=mesh['dp'=16,'tensor'=8] {'dp'}, dimensions={1} | all-to-all | bytes 344064 | tf_op jit(solution)/shard_map/all_to_all | solution.py:94
  24.2 1.1 fusion.36
  25.4 1.1 fusion.35
  26.5 0.0 copy-done
  26.5 0.3 fusion.34
  26.8 1.1 pad_maximum_fusion
  27.9 3.7 %all-to-all-start.1 = ((f32[16,16,1024]{2,1,0:T(8,128)}), f32[16,16,1024]{2,1,0:T(8,128)S(1)}, u32[]{:S(2)}, u32[]{:S(2)}) async-start(f32[16,16,1024]{2,1,0:T(8,128)} %bitcast.3), calls=%async_computation.1 | async-start | bytes 2097152 | tf_op jit(solution)/shard_map/all_to_all | solution.py:22
  31.6 0.0 all-gather.2.cloned.1.call-start
  31.7 0.7 convert_multiply_fusion.2
  32.3 0.7 iota_compare_fusion
  33.1 0.1 multiply_cosine_fusion
  33.2 13.5 %all-to-all-done.1 = f32[16,16,1024]{2,1,0:T(8,128)S(1)} async-done(((f32[16,16,1024]{2,1,0:T(8,128)}), f32[16,16,1024]{2,1,0:T(8,128)S(1)}, u32[]{:S(2)}, u32[]{:S(2)}) %all-to-all-start.1) | async-done | bytes 1048608 | tf_op jit(solution)/shard_map/all_to_all | solution.py:22
  46.7 0.1 reduce_sum.64
  46.7 0.0 copy-start.3
  46.8 0.1 multiply_reduce_fusion.2
  46.9 0.1 multiply_reduce_fusion.1
  47.0 0.0 copy-done.6
  47.0 0.1 multiply_multiply_fusion.1
  47.1 0.0 copy-done.5
  47.1 0.1 multiply_multiply_fusion
  47.2 0.1 multiply_subtract_fusion.1
  47.3 0.1 multiply_subtract_fusion
  47.4 0.1 fusion.46
  47.5 0.1 fusion.28
  47.6 0.1 fusion.29
  47.8 0.0 copy-start.2
  47.8 5.8 %fusion.33 = (f32[16,2,2]{2,1,0:T(2,128)S(1)}, f32[16,2,2,1024]{3,2,1,0:T(2,128)S(1)}) fusion(bf16[16,2,2,128]{3,2,1,0:T(2,128)(2,1)S(1)} %fusion.28, pred[16,1024]{1,0:T(8,128)(4,1)S(1)} %iota_compare_fusion, bf16[16,1024,256]{2,1,0:T(8,128)(2,1)} %param.22), kind=kOutput, calls=%fused_computation.52 | convolution fusion | flops 16908224 | bytes 8683776 | tf_op jit(solution)/shard_map/bgrd,bjgd->bgrj/dot_general | solution.py:130
  53.6 0.3 fusion.24
  54.0 0.0 copy-start.1
  54.0 0.0 copy-start.4
  54.0 4.7 %fusion.12 = bf16[16,2,2,128]{3,2,1,0:T(2,128)(2,1)S(1)} fusion(f32[16,2,2,1024]{3,2,1,0:T(2,128)S(1)} %get-tuple-element.12, f32[16,2,2]{2,1,0:T(2,128)S(1)} %get-tuple-element.4, f32[16,2,2]{2,1,0:T(2,128)S(1)} %bitcast.66, f32[16,2,128]{2,1,0:T(2,128)S(1)} %reshape.164, f32[16,2,2]{2,1,0:T(2,128)S(1)} %convert_element_type.62, ...), kind=kOutput, calls=%fused_computation.8 | convolution fusion | flops 16941056 | bytes 8684288 | tf_op jit(solution)/shard_map/bgrj,bjgd->bgrd/dot_general | solution.py:138
  58.7 0.0 copy-done.3
  58.8 11.4 %all_to_all.43 = bf16[16,16,512]{2,1,0:T(8,128)(2,1)S(1)} all-to-all(bf16[16,16,512]{2,1,0:T(8,128)(2,1)S(1)} %broadcast_in_dim.12), channel_id=1, replica_groups=mesh['dp'=16,'tensor'=8] {'dp'}, dimensions={0} | all-to-all | bytes 524288 | tf_op jit(solution)/shard_map/all_to_all | solution.py:28
  70.2 0.0 copy-done.2
  70.2 0.3 fusion.22
  70.5 11.3 %all_to_all.44 = f32[16,16,336]{2,1,0:T(8,128)S(1)} all-to-all(f32[16,16,336]{2,1,0:T(8,128)S(1)} %fusion.22), channel_id=1, replica_groups=mesh['dp'=16,'tensor'=8] {'dp'}, dimensions={0} | all-to-all | bytes 688128 | tf_op jit(solution)/shard_map/all_to_all | solution.py:147
  81.9 0.1 copy.31
  82.0 0.9 all_gather.6
  83.0 0.0 all-gather.2.cloned.1.call-update
  83.0 0.1 maximum_convert_fusion
  83.1 0.6 copy.60
  83.7 29.2 %all-gather.2.cloned.1.call-done = f32[8,16,5376]{2,1,0:T(8,128)} async-done(((f32[1,16,5376]{2,1,0:T(8,128)}), f32[8,16,5376]{2,1,0:T(8,128)}) %all-gather.2.cloned.1.call-update) | async-done | bytes 2752528 | tf_op jit(solution)/shard_map/all_gather | solution.py:45
  112.9 2.0 %reduce_sum.68 = f32[16,5376]{1,0:T(8,128)S(1)} reduce(f32[8,16,5376]{2,1,0:T(8,128)} %all-gather.2.cloned.1.call-done, f32[]{:T(128)} %constant.9.clone.1), dimensions={0}, to_apply=%region_6.7 | reduce | flops 602112 | bytes 3096580 | tf_op jit(solution)/shard_map/reduce_sum | solution.py:45
  114.8 0.2 multiply_reduce_fusion
  115.0 0.0 copy-done.1
  115.0 0.0 copy-done.4
  115.0 0.8 fusion.21
  (17 shorter events, 0.2 us)
Async XLA Ops:
  7.2 19.4 %copy-start = (bf16[336,512]{1,0:T(8,128)(2,1)S(1)}, bf16[336,512]{1,0:T(8,128)(2,1)}, u32[]{:S(2)}) copy-start(bf16[336,512]{1,0:T(8,128)(2,1)} %param.17) | copy-start | bytes 1032196
  7.2 39.9 %copy-start.6 = (f32[128]{0:T(128)S(1)}, f32[128]{0:T(128)}, u32[]{:S(2)}) copy-start(f32[128]{0:T(128)} %param.21) | copy-start | bytes 1540
  7.2 39.9 %copy-start.5 = (f32[128]{0:T(128)S(1)}, f32[128]{0:T(128)}, u32[]{:S(2)}) copy-start(f32[128]{0:T(128)} %param.20) | copy-start | bytes 1540
  27.9 18.7 %all-to-all-start.1 = ((f32[16,16,1024]{2,1,0:T(8,128)}), f32[16,16,1024]{2,1,0:T(8,128)S(1)}, u32[]{:S(2)}, u32[]{:S(2)}) async-start(f32[16,16,1024]{2,1,0:T(8,128)} %bitcast.3), calls=%async_computation.1 | async-start | bytes 2097152 | tf_op jit(solution)/shard_map/all_to_all | solution.py:22
  31.6 81.3 %all-gather.2.cloned.1.call-start = ((), (), s32[]{:S(2)}) async-start(), calls=%async_computation.4 | async-start | bytes 3096576 | tf_op jit(solution)/shard_map/all_gather | solution.py:45
  46.7 12.0 %copy-start.3 = (bf16[16,256]{1,0:T(8,128)(2,1)}, bf16[16,256]{1,0:T(8,128)(2,1)S(1)}, u32[]{:S(2)}) copy-start(bf16[16,256]{1,0:T(8,128)(2,1)S(1)} %slice.45) | copy-start | bytes 24580
  47.8 22.4 %copy-start.2 = (bf16[512,336]{0,1:T(8,128)(2,1)S(1)}, bf16[512,336]{0,1:T(8,128)(2,1)}, u32[]{:S(2)}) copy-start(bf16[512,336]{0,1:T(8,128)(2,1)} %param.24) | copy-start | bytes 1032196
  54.0 61.0 %copy-start.1 = (bf16[16,5376]{1,0:T(8,128)(2,1)S(1)}, bf16[16,5376]{1,0:T(8,128)(2,1)}, u32[]{:S(2)}) copy-start(bf16[16,5376]{1,0:T(8,128)(2,1)} %param.13) | copy-start | bytes 516100
  54.0 61.0 %copy-start.4 = (f32[5376]{0:T(1024)S(1)}, f32[5376]{0:T(1024)}, u32[]{:S(2)}) copy-start(f32[5376]{0:T(1024)} %param.25) | copy-start | bytes 64516
Sparse Core Ops, SparseCore 0:
  83.1 29.7 all-gather.1
where the time goes:
time: 123 us
  waiting for transfers between devices  42.7 us (35%)
  blocking collectives  37.3 us (30%)
  between operations  14.4 us (12%)
  matrix products  13.5 us (11%)
  other arithmetic  8.94 us (7%)
  starting transfers between devices  3.69 us (3%)
  local copies, waits for them, and re-layouts  2.15 us (2%)
    all_gather x1, waiting for transfers between devices, gathered_total(): return lax.all_gather(array, axis).sum(0)  29.2 us
    all_to_all x1, blocking collectives, per_device(): lax.all_to_all(normed, 'dp', split_axis=1, concat_axis=0, tiled=True)  14.5 us
    all_to_all x1, waiting for transfers between devices, summed_on_arrival(): lax.all_to_all(cut_along(array, dim, peers), axis, 0, 0, tiled=True)  13.5 us
    all_to_all x1, blocking collectives, copy_for_each(): lax.all_to_all(jnp.broadcast_to(array[None], (peers, *array.shape)), axis...  11.4 us
    all_to_all x1, blocking collectives, per_device(): lax.all_to_all(products, 'dp', split_axis=0, concat_axis=1, tiled=True)  11.3 us
    dot_general x1, matrix products, per_device(): jnp.einsum('bgrd,bjgd->bgrj', grouped, cache_keys, preferred_element_type...  5.79 us
    dot_general x1, matrix products, per_device(): jnp.einsum('bgrj,bjgd->bgrd', weights.astype(jnp.bfloat16), cache_values,...  4.72 us
    all_to_all x1, starting transfers between devices, summed_on_arrival(): lax.all_to_all(cut_along(array, dim, peers), axis, 0, 0, tiled=True)  3.65 us
  transfers between devices with their start and end apart: 2, of which 2 were waited for; matrix products, arithmetic and copies ran while one was open for 2% of the time, Pallas kernels for 0%

commit v1 on v0

v1 whole, which is shorter than its diff:
```python
import functools

import jax
import jax.numpy as jnp
import numpy as np
from jax import lax
from jax.experimental import pallas as pl
from jax.experimental.pallas import tpu as pltpu
from jax.sharding import PartitionSpec as P

HD = 128
QPRE = 168
LANES = 128
EPS = 1e-06
ROPE_BASE = 1000000.0
ROPE_FACTOR = 8.0
MESH = pl.DeviceIdType.MESH
F32 = jnp.float32
BF16 = jnp.bfloat16


def padded(width):
    return -(-width // LANES) * LANES


def ring_distance(step, size):
    return min(step % size, -step % size)


def plane_offsets(side):
    steps = [(a, b) for a in range(side) for b in range(side)]
    return sorted(steps, key=lambda s: (ring_distance(s[0], side) + ring_distance(s[1], side), s))


def line_offsets(depth):
    steps = [(a, c) for a in range(depth) for c in range(2)]
    return sorted(steps, key=lambda s: (ring_distance(s[0], depth), s[1]))


def kernel(
    dims,
    tokens_hbm, lengths_hbm, positions_hbm, in_gain_hbm, qw_hbm, kw_hbm, vw_hbm, q_gain_hbm, k_gain_hbm,
    kc_hbm, vc_hbm, ow_hbm, post_gain_hbm, freq_hbm,
    hid_hbm, nk_out, nv_out,
    tokens, lengths, positions, in_gain, weights, q_gain, k_gain, kcache, vcache, oweight, post_gain, freq,
    normed, tok_mine, slots, spread, part_out, part_in, scores, probs, att_in, prod, red_out, red_in,
    proj_out, proj_in, row_out,
    load_sem, cache_sem, s1, r1, s2, r2, s3, r3, s4, r4, s5, r5, s6, r6, last_sem,
):
    dp, tensor, side, rows, width, share, q_cols, kv_cols, ctx = dims
    depth = tensor // 2
    mine = rows // tensor
    heads = q_cols // HD
    kv_heads = kv_cols // HD
    per_kv = heads // kv_heads
    share_pad = padded(share)
    me = lax.axis_index("dp")
    me_t = lax.axis_index("tensor")
    my_x, my_y = me // side, me % side
    my_z, my_c = me_t // 2, me_t % 2

    def plane_peer(step):
        return ((my_x + step[0]) % side) * side + (my_y + step[1]) % side

    def plane_source(step):
        return ((my_x + side - step[0]) % side) * side + (my_y + side - step[1]) % side

    def line_peer(step):
        return ((my_z + step[0]) % depth) * 2 + (my_c + step[1]) % 2

    plane = plane_offsets(side)
    line = line_offsets(depth)

    def load(src, dst, at):
        copy = pltpu.make_async_copy(src, dst, load_sem.at[at])
        copy.start()
        return copy

    c_tokens = load(tokens_hbm, tokens, 0)
    c_gain = load(in_gain_hbm, in_gain, 1)
    c_w = [
        load(qw_hbm, weights.at[pl.ds(0, share), pl.ds(0, q_cols)], 2),
        load(kw_hbm, weights.at[pl.ds(0, share), pl.ds(q_cols, kv_cols)], 3),
        load(vw_hbm, weights.at[pl.ds(0, share), pl.ds(q_cols + kv_cols, kv_cols)], 4),
    ]
    c_small = [
        load(lengths_hbm, lengths, 5), load(positions_hbm, positions, 6), load(q_gain_hbm, q_gain, 7),
        load(k_gain_hbm, k_gain, 8), load(post_gain_hbm, post_gain, 9), load(freq_hbm, freq, 10),
    ]
    c_ow = load(ow_hbm, oweight, 11)

    barrier = pltpu.get_barrier_semaphore()
    for step in plane[1:]:
        pl.semaphore_signal(barrier, inc=1, device_id={"dp": plane_peer(step)}, device_id_type=MESH)
    for step in line[1:]:
        pl.semaphore_signal(barrier, inc=1, device_id={"tensor": line_peer(step)}, device_id_type=MESH)

    c_k, c_v = [], []
    for b in range(rows):
        copy = pltpu.make_async_copy(kc_hbm.at[b], kcache.at[b], cache_sem.at[0, b])
        copy.start()
        c_k.append(copy)
    for b in range(rows):
        copy = pltpu.make_async_copy(vc_hbm.at[b], vcache.at[b], cache_sem.at[1, b])
        copy.start()
        c_v.append(copy)

    c_tokens.wait()
    c_gain.wait()
    x = tokens[...].astype(F32)
    mean_square = jnp.sum(x * x, axis=1, keepdims=True) * (1.0 / width)
    normed[:, :width] = x * lax.rsqrt(mean_square + EPS) * in_gain[...]
    normed[:, width:] = jnp.zeros((rows, normed.shape[1] - width), F32)
    for d in range(dp):
        first = share * d
        low = first // LANES * LANES
        window = normed[:, low : low + share_pad + LANES]
        if first != low:
            window = pltpu.roll(window, window.shape[1] - (first - low), 1)
        slots[d] = window[:, :share_pad].astype(BF16)

    pl.semaphore_wait(barrier, len(plane) + len(line) - 2)

    sends = []

    def send(src, dst, send_sem, recv_sem, device):
        copy = pltpu.make_async_remote_copy(
            src_ref=src, dst_ref=dst, send_sem=send_sem, recv_sem=recv_sem, device_id=device, device_id_type=MESH
        )
        copy.start()
        sends.append(copy)
        return copy

    first_copies = [None] * dp
    for k in range(1, dp):
        peer = plane_peer(plane[k])
        first_copies[k] = send(slots.at[peer], spread.at[k], s1.at[k], r1.at[k], {"dp": peer})
    spread[0] = slots[me]

    weights[share:, :] = jnp.zeros((share_pad - share, weights.shape[1]), BF16)
    for copy in c_small:
        copy.wait()
    sub = lax.broadcasted_iota(jnp.int32, (rows, rows), 0)
    lane = lax.broadcasted_iota(jnp.int32, (rows, rows), 1)
    pos_col = jnp.sum(jnp.where(sub == lane, positions[...].astype(F32), 0.0), axis=1, keepdims=True)
    angles = (pos_col * (1.0 / ROPE_FACTOR)) * freq[...]
    cos_part = jnp.cos(angles)
    half = lax.broadcasted_iota(jnp.int32, (rows, HD), 1) < HD // 2
    sin_part = jnp.where(half, -jnp.sin(angles), jnp.sin(angles))
    len_row = jnp.concatenate([lengths[...]] * heads + [jnp.zeros((1, HD // 2 - heads * rows), jnp.int32)] * (heads * rows < HD // 2), axis=1)
    len_row = jnp.concatenate([len_row, len_row], axis=1)
    own_rows = lax.broadcasted_iota(jnp.int32, (rows, LANES), 0)
    for tile in range(width // LANES):
        block = tokens[:, tile * LANES : (tile + 1) * LANES].astype(F32)
        for i in range(mine):
            tok_mine[i : i + 1, tile * LANES : (tile + 1) * LANES] = jnp.sum(
                jnp.where(own_rows == me_t * mine + i, block, 0.0), axis=0, keepdims=True
            )
    for copy in c_w:
        copy.wait()

    group = max(dp // 4, 1)
    own_part = None
    second_copies = [None] * dp
    for g0 in range(0, dp, group):
        for k in range(max(g0, 1), g0 + group):
            first_copies[k].wait_recv()
        lhs = spread[g0 : g0 + group].reshape(group * rows, share_pad)
        part = jnp.dot(lhs, weights[...], preferred_element_type=F32)
        if g0 == 0:
            own_part = part[:rows]
        part_out[g0 : g0 + group] = part.astype(BF16).reshape(group, rows, part.shape[1])
        for k in range(max(g0, 1), g0 + group):
            second_copies[k] = send(
                part_out.at[k], part_in.at[k], s2.at[k], r2.at[k], {"dp": plane_source(plane[k])}
            )

    joined = own_part
    for k in range(1, dp):
        second_copies[k].wait_recv()
        joined = joined + part_in[k].astype(F32)

    def rms_rope(vectors, gain):
        square = jnp.sum(vectors * vectors, axis=1, keepdims=True) * (1.0 / HD)
        scaled = vectors * lax.rsqrt(square + EPS) * gain
        return scaled * cos_part + pltpu.roll(scaled, HD // 2, 1) * sin_part

    queries = [
        (rms_rope(joined[:, h * HD : (h + 1) * HD], q_gain[...]) * QPRE ** (-0.5)).astype(BF16) for h in range(heads)
    ]
    new_keys = jnp.concatenate(
        [rms_rope(joined[:, q_cols + g * HD : q_cols + (g + 1) * HD], k_gain[...]) for g in range(kv_heads)], axis=1
    ).astype(BF16)
    new_values = joined[:, q_cols + kv_cols :].astype(BF16)
    nk_out[...] = new_keys
    nv_out[...] = new_values

    zero_head = jnp.zeros((rows, HD), BF16)
    stacked = [
        jnp.concatenate([queries[h] if g == h // per_kv else zero_head for g in range(kv_heads)], axis=1)
        for h in range(heads)
    ]
    used = heads * rows
    if used < HD // 2:
        stacked.append(jnp.zeros((HD // 2 - used, kv_cols), BF16))
    query_rows = jnp.concatenate(stacked, axis=0)
    half_rows = HD // 2
    query_of = lax.broadcasted_iota(jnp.int32, (half_rows, 1), 0) % rows
    zeros_half = jnp.zeros((half_rows, kv_cols), BF16)
    picks = [(query_of == b).astype(F32).astype(BF16) for b in range(rows)]
    contract_last = (((1,), (1,)), ((), ()))
    for copy in c_k:
        copy.wait()
    slots_half = ctx // 2
    block_rows = min(256, slots_half)
    blocks = slots_half // block_rows
    low_q, high_q = [], []
    for b in range(rows):
        only = query_rows * picks[b]
        low_q.append(jnp.concatenate([only, zeros_half], axis=0))
        high_q.append(jnp.concatenate([zeros_half, only], axis=0))
    lane_row = lax.broadcasted_iota(jnp.int32, (1, HD), 1)
    base_slot = jnp.where(lane_row < half_rows, 0, slots_half)
    largest = None
    for m in range(blocks):
        total = None
        for b in range(rows):
            low = lax.dot_general(
                kcache[b, m * block_rows : (m + 1) * block_rows, :], low_q[b], contract_last, preferred_element_type=F32
            )
            high = lax.dot_general(
                kcache[b, slots_half + m * block_rows : slots_half + (m + 1) * block_rows, :], high_q[b],
                contract_last, preferred_element_type=F32,
            )
            total = low + high if total is None else total + low + high
        slot = lax.broadcasted_iota(jnp.int32, (block_rows, HD), 0) + (m * block_rows) + base_slot
        total = jnp.where(slot < len_row, total, -jnp.inf)
        scores[m * block_rows : (m + 1) * block_rows, :] = total
        top = jnp.max(total, axis=0, keepdims=True)
        largest = top if largest is None else jnp.maximum(largest, top)
    own_scores = lax.dot_general(
        new_keys, jnp.concatenate([query_rows, query_rows], axis=0), contract_last, preferred_element_type=F32
    )
    own_lane = lax.broadcasted_iota(jnp.int32, (rows, HD), 1) % rows
    own_diag = lax.broadcasted_iota(jnp.int32, (rows, HD), 0) == own_lane
    own_row = jnp.sum(jnp.where(own_diag, own_scores, 0.0), axis=0, keepdims=True)
    largest = jnp.maximum(jnp.maximum(largest, pltpu.roll(largest, half_rows, 1)), own_row)
    own_weight = jnp.exp(own_row - largest)
    total_row = None
    for m in range(blocks):
        weight = jnp.exp(scores[m * block_rows : (m + 1) * block_rows, :] - largest)
        part_total = jnp.sum(weight, axis=0, keepdims=True)
        total_row = part_total if total_row is None else total_row + part_total
        probs[:, m * block_rows : (m + 1) * block_rows] = weight.T.astype(BF16)
    total_row = total_row + pltpu.roll(total_row, half_rows, 1) + own_weight
    eye = lax.broadcasted_iota(jnp.int32, (half_rows, HD), 0) == lax.broadcasted_iota(jnp.int32, (half_rows, HD), 1)
    total_col = jnp.sum(jnp.where(eye, total_row, 0.0), axis=1, keepdims=True)
    own_block = jnp.where(own_diag, own_weight, 0.0)[:, :half_rows].astype(BF16)
    mixture = lax.dot_general(own_block, new_values, (((0,), (0,)), ((), ())), preferred_element_type=F32)
    for copy in c_v:
        copy.wait()
    low_p = probs[:half_rows, :]
    high_p = probs[half_rows:, :]
    for b in range(rows):
        mixture = mixture + jnp.dot(low_p * picks[b], vcache[b, :slots_half, :], preferred_element_type=F32)
        mixture = mixture + jnp.dot(high_p * picks[b], vcache[b, slots_half:, :], preferred_element_type=F32)
    mixture = mixture / total_col
    attended = jnp.concatenate(
        [mixture[h * rows : (h + 1) * rows, (h // per_kv) * HD : (h // per_kv + 1) * HD] for h in range(heads)], axis=1
    ).astype(BF16)

    att_in[0] = attended
    third_copies = [None] * dp
    for k in range(1, dp):
        third_copies[k] = send(att_in.at[0], att_in.at[k], s3.at[k], r3.at[k], {"dp": plane_peer(plane[k])})
    c_ow.wait()
    for k in range(1, dp):
        third_copies[k].wait_recv()
    products = lax.dot_general(
        att_in[...].reshape(dp * rows, q_cols), oweight[...], contract_last, preferred_element_type=F32
    )
    products = jnp.concatenate([products, jnp.zeros((dp * rows, share_pad - share), F32)], axis=1)
    for c in range(share_pad // LANES):
        prod[c] = products[:, c * LANES : (c + 1) * LANES]

    for t in range(tensor):
        for i in range(mine):
            for c in range(share_pad // LANES):
                red_out[t, i, :, c * LANES : (c + 1) * LANES] = prod[c, pl.ds(mine * t + i, dp, rows), :].astype(BF16)
    fourth_copies = [None] * tensor
    for k in range(1, tensor):
        peer = line_peer(line[k])
        fourth_copies[k] = send(red_out.at[peer], red_in.at[k], s4.at[k], r4.at[k], {"tensor": peer})
    red_in[0] = red_out[me_t]
    for k in range(1, tensor):
        fourth_copies[k].wait_recv()
    shift = lax.rem(me * share, LANES)
    lanes_of = lax.broadcasted_iota(jnp.int32, (dp, LANES), 1)
    for i in range(mine):
        summed = red_in[0, i].astype(F32)
        for k in range(1, tensor):
            summed = summed + red_in[k, i].astype(F32)
        turned = [
            pltpu.roll(summed[:, c * LANES : (c + 1) * LANES], shift, 1) for c in range(share_pad // LANES)
        ]
        none = jnp.zeros((dp, LANES), F32)
        window = jnp.concatenate(
            [jnp.where(lanes_of < shift, before, after) for before, after in zip([none] + turned, turned + [none])],
            axis=1,
        )
        for k in range(dp):
            proj_out[k, i : i + 1, :] = window[k : k + 1, :]

    fifth_copies = [None] * dp
    for k in range(1, dp):
        fifth_copies[k] = send(
            proj_out.at[k], proj_in.at[me], s5.at[k], r5.at[k], {"dp": plane_source(plane[k])}
        )
    proj_in[me] = proj_out[0]
    for k in range(1, dp):
        fifth_copies[k].wait_recv()
    tiles = [jnp.zeros((mine, LANES), F32) for _ in range(width // LANES)]
    for d in range(dp):
        first = share * d
        low = first // LANES
        for c in range((first + share - 1) // LANES - low + 1):
            tiles[low + c] = tiles[low + c] + proj_in[d, :, c * LANES : (c + 1) * LANES]
    square = tiles[0] * tiles[0]
    for tile in tiles[1:]:
        square = square + tile * tile
    scale = lax.rsqrt(jnp.sum(square, axis=1, keepdims=True) * (1.0 / width) + EPS)
    projected = jnp.concatenate(tiles, axis=1)
    row_out[...] = (tok_mine[...] + projected * scale * post_gain[...]).astype(BF16)

    keep = pltpu.make_async_copy(row_out, hid_hbm.at[me_t], last_sem)
    keep.start()
    sixth_copies = [None] * tensor
    for k in range(1, tensor):
        sixth_copies[k] = send(
            row_out, hid_hbm.at[me_t], s6.at[k], r6.at[k], {"tensor": line_peer(line[k])}
        )
    for k in range(1, tensor):
        sixth_copies[k].wait_recv()
    keep.wait()
    for copy in sends:
        copy.wait_send()


def per_device(dp, tensor, side, *args):
    tokens, lengths, positions, in_gain, qw, kw, vw, q_gain, k_gain, kc, vc, ow, post_gain = args
    rows, width = tokens.shape
    share, q_cols = qw.shape
    kv_cols = kw.shape[1]
    ctx = kc.shape[1]
    share_pad = padded(share)
    cols = q_cols + 2 * kv_cols
    mine = rows // tensor
    dims = (dp, tensor, side, rows, width, share, q_cols, kv_cols, ctx)
    exponent = np.arange(HD // 2, dtype=np.float64) * (2.0 / HD)
    frequency = (ROPE_BASE**-exponent).astype(np.float32)
    freq = jnp.asarray(np.concatenate([frequency, frequency])[None])
    any_spec = pl.BlockSpec(memory_space=pl.ANY)
    vmem_spec = pl.BlockSpec(memory_space=pltpu.VMEM)
    dma = pltpu.SemaphoreType.DMA
    hidden, new_keys, new_values = pl.pallas_call(
        functools.partial(kernel, dims),
        out_shape=(
            jax.ShapeDtypeStruct((tensor, mine, width), BF16),
            jax.ShapeDtypeStruct((rows, kv_cols), BF16),
            jax.ShapeDtypeStruct((rows, kv_cols), BF16),
        ),
        in_specs=[any_spec] * 14,
        out_specs=(any_spec, vmem_spec, vmem_spec),
        scratch_shapes=[
            pltpu.VMEM((rows, width), BF16),
            pltpu.VMEM((1, rows), jnp.int32),
            pltpu.VMEM((1, rows), jnp.int32),
            pltpu.VMEM((1, width), F32),
            pltpu.VMEM((share_pad, cols), BF16),
            pltpu.VMEM((1, HD), F32),
            pltpu.VMEM((1, HD), F32),
            pltpu.VMEM((rows, ctx, kv_cols), BF16),
            pltpu.VMEM((rows, ctx, kv_cols), BF16),
            pltpu.VMEM((share, q_cols), BF16),
            pltpu.VMEM((1, width), F32),
            pltpu.VMEM((1, HD), F32),
            pltpu.VMEM((rows, width + 2 * LANES), F32),
            pltpu.VMEM((mine, width), F32),
            pltpu.VMEM((dp, rows, share_pad), BF16),
            pltpu.VMEM((dp, rows, share_pad), BF16),
            pltpu.VMEM((dp, rows, cols), BF16),
            pltpu.VMEM((dp, rows, cols), BF16),
            pltpu.VMEM((ctx // 2, HD), F32),
            pltpu.VMEM((HD, ctx // 2), BF16),
            pltpu.VMEM((dp, rows, q_cols), BF16),
            pltpu.VMEM((share_pad // LANES, dp * rows, LANES), F32),
            pltpu.VMEM((tensor, mine, dp, share_pad), BF16),
            pltpu.VMEM((tensor, mine, dp, share_pad), BF16),
            pltpu.VMEM((dp, mine, share_pad + LANES), F32),
            pltpu.VMEM((dp, mine, share_pad + LANES), F32),
            pltpu.VMEM((mine, width), BF16),
            dma((12,)),
            dma((2, rows)),
            dma((dp,)), dma((dp,)),
            dma((dp,)), dma((dp,)),
            dma((dp,)), dma((dp,)),
            dma((tensor,)), dma((tensor,)),
            dma((dp,)), dma((dp,)),
            dma((tensor,)), dma((tensor,)),
            dma(()),
        ],
        compiler_params=pltpu.CompilerParams(collective_id=0, has_side_effects=True),
    )(
        tokens, lengths.reshape(1, rows), positions.reshape(1, rows), in_gain.reshape(1, width), qw, kw, vw,
        q_gain.reshape(1, HD), k_gain.reshape(1, HD), kc, vc, ow.T, post_gain.reshape(1, width), freq,
    )
    return hidden.reshape(rows, width), new_keys, new_values


def solution(mesh):
    dp, tensor = mesh.shape["dp"], mesh.shape["tensor"]
    side = int(round(dp**0.5))
    return jax.shard_map(
        functools.partial(per_device, dp, tensor, side),
        mesh=mesh,
        in_specs=(
            P("dp", None), P("dp"), P("dp"), P(), P("dp", "tensor"), P("dp", "tensor"), P("dp", "tensor"), P(), P(),
            P("dp", None, "tensor"), P("dp", None, "tensor"), P("tensor", "dp"), P(),
        ),
        out_specs=(P("dp", None), P("dp", "tensor"), P("dp", "tensor")),
        check_vma=False,
    )
```

time: 123 us -> 57.5 us (0.47)
  Pallas kernels: 0 us -> 49.5 us
  waiting for transfers between devices: 42.7 us -> 0 us
  blocking collectives: 37.3 us -> 0 us
  between operations: 14.4 us -> 0.64 us
  matrix products: 13.5 us -> 0 us
  other arithmetic: 8.94 us -> 0 us
  local copies, waits for them, and re-layouts: 2.15 us -> 6.96 us
  starting transfers between devices: 3.69 us -> 0 us
    pallas_call x0 -> x1, Pallas kernels: none -> 49.5 us  [per_device(): pl.pallas_call(functools.partial(kernel, dims), out_shape=(jax.ShapeDtype...]
    all_to_all x3 -> x0, blocking collectives: 37.3 us -> none  [the longest x1 14.5 us: per_device(): lax.all_to_all(normed, 'dp', split_axis=1, concat_axis=0, tiled=True)]
    all_gather x1 -> x0, waiting for transfers between devices: 29.2 us -> none  [gathered_total(): return lax.all_gather(array, axis).sum(0)]
    dot_general x7 -> x0, matrix products: 13.5 us -> none  [the longest x1 5.79 us: per_device(): jnp.einsum('bgrd,bjgd->bgrj', grouped, cache_keys, preferred_element_type...]
    all_to_all x1 -> x0, waiting for transfers between devices: 13.5 us -> none  [summed_on_arrival(): lax.all_to_all(cut_along(array, dim, peers), axis, 0, 0, tiled=True)]
    reshape x2 -> x3, local copies, waits for them, and re-layouts: 0.03 us -> 4.37 us  [the longest x1 1.65 us: per_device(): return (hidden.reshape(rows, width), new_keys, new_values)]
    reduce_sum x7 -> x0, other arithmetic: 3.8 us -> none  [the longest x1 1.95 us: gathered_total(): return lax.all_gather(array, axis).sum(0)]
    all_to_all x1 -> x0, starting transfers between devices: 3.65 us -> none  [summed_on_arrival(): lax.all_to_all(cut_along(array, dim, peers), axis, 0, 0, tiled=True)]
  transfers between devices with their start and end apart: 2 -> 0, of which waited for: 2 -> 0; matrix products, arithmetic and copies ran while one was open for 2% -> 0% of each run, Pallas kernels for 0% -> 0%
where the time goes in v1:
time: 57.5 us; the launch traced here: 57.1 us
  Pallas kernels  49.5 us (86%)
  local copies, waits for them, and re-layouts  6.96 us (12%)
  between operations  0.64 us (1%)
    pallas_call x1, Pallas kernels, per_device(): pl.pallas_call(functools.partial(kernel, dims), out_shape=(jax.ShapeDtype...  49.5 us
    unnamed x2, local copies, waits for them, and re-layouts  2.59 us
    reshape x1, local copies, waits for them, and re-layouts, per_device(): return (hidden.reshape(rows, width), new_keys, new_values)  1.65 us
    reshape x1, local copies, waits for them, and re-layouts, per_device(): in_gain.reshape(1, width)  1.36 us
    reshape x1, local copies, waits for them, and re-layouts, per_device(): post_gain.reshape(1, width)  1.35 us

profile of v1, /device:TPU:1, one launch (start us, length us, event | category | flops | bytes accessed | tf_op | source)
XLA Modules:
  0.0 57.1 jit_solution(13764369539829438217)
XLA Ops:
  0.6 1.4 %reshape.29.in_gain_hbm = f32[1,5376]{1,0:T(1,128)} reshape(f32[5376]{0:T(1024)} %param.17) | data formatting | bytes 43008 | tf_op jit(solution)/shard_map/reshape | solution.py:414
  2.0 1.4 %reshape.32.post_gain_hbm = f32[1,5376]{1,0:T(1,128)} reshape(f32[5376]{0:T(1024)} %param.26) | data formatting | bytes 43008 | tf_op jit(solution)/shard_map/reshape | solution.py:415
  3.3 49.5 %shard_map.157 = (bf16[8,2,5376]{2,1,0:T(2,128)(2,1)}, bf16[16,256]{1,0:T(8,128)(2,1)}, bf16[16,256]{1,0:T(8,128)(2,1)}) custom-call(bf16[16,5376]{1,0:T(8,128)(2,1)} %tokens_hbm.1, s32[1,16]{1,0:T(1,128)} %bitcast.6, s32[1,16]{1,0:T(1,128)} %bitcast.7, f32[1,5376]{1,0:T(1,128)} %reshape.29.in_gain_hbm, bf16[336,512]{1,0:T(8,128)(2,1)} %qw_hbm.1, ...), custom_call_target="tpu_custom_call" | custom-call | tf_op jit(solution)/shard_map/pallas_call | solution.py:365
  52.9 1.7 %reshape.33 = bf16[16,5376]{1,0:T(8,128)(2,1)} reshape(bf16[8,2,5376]{2,1,0:T(2,128)(2,1)} %get-tuple-element.6) | data formatting | bytes 344064 | tf_op jit(solution)/shard_map/reshape | solution.py:417
  54.6 1.3 %copy.19 = bf16[16,256]{1,0:T(8,128)(2,1)} copy(bf16[16,256]{1,0:T(8,128)(2,1)} %get-tuple-element.13) | data formatting | bytes 16384
  55.9 1.3 %copy.20 = bf16[16,256]{1,0:T(8,128)(2,1)} copy(bf16[16,256]{1,0:T(8,128)(2,1)} %get-tuple-element.14) | data formatting | bytes 16384

commit v2 on v1

--- a/solution.py
+++ b/solution.py
@@ -43,11 +43,10 @@
     kc_hbm, vc_hbm, ow_hbm, post_gain_hbm, freq_hbm,
     hid_hbm, nk_out, nv_out,
     tokens, lengths, positions, in_gain, weights, q_gain, k_gain, kcache, vcache, oweight, post_gain, freq,
-    normed, tok_mine, slots, spread, part_out, part_in, scores, probs, att_in, prod, red_out, red_in,
-    proj_out, proj_in, row_out,
-    load_sem, cache_sem, s1, r1, s2, r2, s3, r3, s4, r4, s5, r5, s6, r6, last_sem,
+    normed, tok_mine, slots, spread, part_out, part_in, scores, probs, att_in, red_out, red_in, row_out,
+    load_sem, cache_sem, s1, r1, s2, r2, s3, r3, s4, r4, s5, r5, sw, rw, last_sem,
 ):
-    dp, tensor, side, rows, width, share, q_cols, kv_cols, ctx = dims
+    dp, tensor, side, rows, width, share, q_cols, kv_cols, ctx, strip = dims
     depth = tensor // 2
     mine = rows // tensor
     heads = q_cols // HD
@@ -56,20 +55,41 @@
     share_pad = padded(share)
     me = lax.axis_index("dp")
     me_t = lax.axis_index("tensor")
-    my_x, my_y = me // side, me % side
-    my_z, my_c = me_t // 2, me_t % 2
+    my_x, my_y = lax.div(me, side), lax.rem(me, side)
+    my_z, my_c = lax.div(me_t, 2), lax.rem(me_t, 2)
+    xs = [my_x] + [lax.rem(my_x + a, side) for a in range(1, side)]
+    ys = [my_y] + [lax.rem(my_y + a, side) for a in range(1, side)]
+    zs = [my_z] + [lax.rem(my_z + a, depth) for a in range(1, depth)]
+    cs = [my_c, 1 - my_c]
 
     def plane_peer(step):
-        return ((my_x + step[0]) % side) * side + (my_y + step[1]) % side
+        return xs[step[0]] * side + ys[step[1]]
 
     def plane_source(step):
-        return ((my_x + side - step[0]) % side) * side + (my_y + side - step[1]) % side
+        return xs[-step[0]] * side + ys[-step[1]]
 
     def line_peer(step):
-        return ((my_z + step[0]) % depth) * 2 + (my_c + step[1]) % 2
+        return zs[step[0]] * 2 + cs[step[1]]
 
     plane = plane_offsets(side)
     line = line_offsets(depth)
+    ring = sorted(range(side), key=lambda a: (ring_distance(a, side), a))
+
+    skew = lax.rem(my_x * (side * share), LANES)
+    edge = strip - side * share
+    oweight[:edge, :] = jnp.zeros((edge, q_cols), BF16)
+    oweight[side * share :, :] = jnp.zeros((edge, q_cols), BF16)
+
+    barrier = pltpu.get_barrier_semaphore()
+    for step in reversed(plane[1:]):
+        pl.semaphore_signal(barrier, inc=1, device_id={"dp": plane_peer(step)}, device_id_type=MESH)
+    for kx, ahead in enumerate(ring):
+        for kt, step in enumerate(line):
+            if kt:
+                pl.semaphore_signal(
+                    barrier, inc=1, device_id={"dp": plane_peer((ahead, 0)), "tensor": line_peer(step)},
+                    device_id_type=MESH,
+                )
 
     def load(src, dst, at):
         copy = pltpu.make_async_copy(src, dst, load_sem.at[at])
@@ -77,7 +97,7 @@
         return copy
 
     c_tokens = load(tokens_hbm, tokens, 0)
-    c_gain = load(in_gain_hbm, in_gain, 1)
+    c_gain = load(in_gain_hbm, in_gain.at[0], 1)
     c_w = [
         load(qw_hbm, weights.at[pl.ds(0, share), pl.ds(0, q_cols)], 2),
         load(kw_hbm, weights.at[pl.ds(0, share), pl.ds(q_cols, kv_cols)], 3),
@@ -85,25 +105,13 @@
     ]
     c_small = [
         load(lengths_hbm, lengths, 5), load(positions_hbm, positions, 6), load(q_gain_hbm, q_gain, 7),
-        load(k_gain_hbm, k_gain, 8), load(post_gain_hbm, post_gain, 9), load(freq_hbm, freq, 10),
+        load(k_gain_hbm, k_gain, 8), load(post_gain_hbm, post_gain.at[0], 9), load(freq_hbm, freq, 10),
     ]
-    c_ow = load(ow_hbm, oweight, 11)
-
-    barrier = pltpu.get_barrier_semaphore()
-    for step in plane[1:]:
-        pl.semaphore_signal(barrier, inc=1, device_id={"dp": plane_peer(step)}, device_id_type=MESH)
-    for step in line[1:]:
-        pl.semaphore_signal(barrier, inc=1, device_id={"tensor": line_peer(step)}, device_id_type=MESH)
-
-    c_k, c_v = [], []
-    for b in range(rows):
-        copy = pltpu.make_async_copy(kc_hbm.at[b], kcache.at[b], cache_sem.at[0, b])
-        copy.start()
-        c_k.append(copy)
-    for b in range(rows):
-        copy = pltpu.make_async_copy(vc_hbm.at[b], vcache.at[b], cache_sem.at[1, b])
-        copy.start()
-        c_v.append(copy)
+    def rows_of(y, first, count):
+        return oweight.at[pl.ds(pl.multiple_of(skew + y * share + first, 16), count), :]
+
+    own_block = rows_of(my_y, 0, share)
+    c_ow = load(ow_hbm, own_block, 11)
 
     c_tokens.wait()
     c_gain.wait()
@@ -119,7 +127,7 @@
             window = pltpu.roll(window, window.shape[1] - (first - low), 1)
         slots[d] = window[:, :share_pad].astype(BF16)
 
-    pl.semaphore_wait(barrier, len(plane) + len(line) - 2)
+    pl.semaphore_wait(barrier, dp - 1 + side * (tensor - 1))
 
     sends = []
 
@@ -136,6 +144,23 @@
         peer = plane_peer(plane[k])
         first_copies[k] = send(slots.at[peer], spread.at[k], s1.at[k], r1.at[k], {"dp": peer})
     spread[0] = slots[me]
+    early = -(-share // 32) * 16
+    ways = ((1, 0, early), (side - 1, share - early, 0))
+    c_ow.wait()
+    early_copies = []
+    for way, (step, first, _) in enumerate(ways):
+        piece = rows_of(my_y, first, early)
+        early_copies.append(send(piece, piece, sw.at[way, 0], rw.at[way, 0], {"dp": plane_peer((0, step))}))
+
+    c_k, c_v = [], []
+    for b in range(rows):
+        copy = pltpu.make_async_copy(kc_hbm.at[b], kcache.at[b], cache_sem.at[0, b])
+        copy.start()
+        c_k.append(copy)
+    for b in range(rows):
+        copy = pltpu.make_async_copy(vc_hbm.at[b], vcache.at[b], cache_sem.at[1, b])
+        copy.start()
+        c_v.append(copy)
 
     weights[share:, :] = jnp.zeros((share_pad - share, weights.shape[1]), BF16)
     for copy in c_small:
@@ -179,6 +204,15 @@
     for k in range(1, dp):
         second_copies[k].wait_recv()
         joined = joined + part_in[k].astype(F32)
+
+    late_copies = []
+    for copy in early_copies:
+        copy.wait_recv()
+    for way, (step, first, rest) in enumerate(ways):
+        piece = rows_of(ys[-step], way * early, early if way == 0 else share - early)
+        late_copies.append(send(piece, piece, sw.at[way, 1], rw.at[way, 1], {"dp": plane_peer((0, step))}))
+        piece = rows_of(my_y, rest, share - early)
+        late_copies.append(send(piece, piece, sw.at[way, 2], rw.at[way, 2], {"dp": plane_peer((0, step))}))
 
     def rms_rope(vectors, gain):
         square = jnp.sum(vectors * vectors, axis=1, keepdims=True) * (1.0 / HD)
@@ -255,8 +289,8 @@
     total_row = total_row + pltpu.roll(total_row, half_rows, 1) + own_weight
     eye = lax.broadcasted_iota(jnp.int32, (half_rows, HD), 0) == lax.broadcasted_iota(jnp.int32, (half_rows, HD), 1)
     total_col = jnp.sum(jnp.where(eye, total_row, 0.0), axis=1, keepdims=True)
-    own_block = jnp.where(own_diag, own_weight, 0.0)[:, :half_rows].astype(BF16)
-    mixture = lax.dot_general(own_block, new_values, (((0,), (0,)), ((), ())), preferred_element_type=F32)
+    own_mix = jnp.where(own_diag, own_weight, 0.0)[:, :half_rows].astype(BF16)
+    mixture = lax.dot_general(own_mix, new_values, (((0,), (0,)), ((), ())), preferred_element_type=F32)
     for copy in c_v:
         copy.wait()
     low_p = probs[:half_rows, :]
@@ -270,61 +304,44 @@
     ).astype(BF16)
 
     att_in[0] = attended
-    third_copies = [None] * dp
-    for k in range(1, dp):
-        third_copies[k] = send(att_in.at[0], att_in.at[k], s3.at[k], r3.at[k], {"dp": plane_peer(plane[k])})
-    c_ow.wait()
-    for k in range(1, dp):
+    third_copies = [None] * side
+    for k in reversed(range(1, side)):
+        third_copies[k] = send(
+            att_in.at[0], att_in.at[k], s3.at[k], r3.at[k], {"dp": plane_peer((ring[k], 0))}
+        )
+    for copy in late_copies:
+        copy.wait_recv()
+    for k in range(1, side):
         third_copies[k].wait_recv()
     products = lax.dot_general(
-        att_in[...].reshape(dp * rows, q_cols), oweight[...], contract_last, preferred_element_type=F32
-    )
-    products = jnp.concatenate([products, jnp.zeros((dp * rows, share_pad - share), F32)], axis=1)
-    for c in range(share_pad // LANES):
-        prod[c] = products[:, c * LANES : (c + 1) * LANES]
-
-    for t in range(tensor):
-        for i in range(mine):
-            for c in range(share_pad // LANES):
-                red_out[t, i, :, c * LANES : (c + 1) * LANES] = prod[c, pl.ds(mine * t + i, dp, rows), :].astype(BF16)
-    fourth_copies = [None] * tensor
-    for k in range(1, tensor):
-        peer = line_peer(line[k])
-        fourth_copies[k] = send(red_out.at[peer], red_in.at[k], s4.at[k], r4.at[k], {"tensor": peer})
-    red_in[0] = red_out[me_t]
-    for k in range(1, tensor):
-        fourth_copies[k].wait_recv()
-    shift = lax.rem(me * share, LANES)
-    lanes_of = lax.broadcasted_iota(jnp.int32, (dp, LANES), 1)
-    for i in range(mine):
-        summed = red_in[0, i].astype(F32)
-        for k in range(1, tensor):
-            summed = summed + red_in[k, i].astype(F32)
-        turned = [
-            pltpu.roll(summed[:, c * LANES : (c + 1) * LANES], shift, 1) for c in range(share_pad // LANES)
-        ]
-        none = jnp.zeros((dp, LANES), F32)
-        window = jnp.concatenate(
-            [jnp.where(lanes_of < shift, before, after) for before, after in zip([none] + turned, turned + [none])],
-            axis=1,
-        )
-        for k in range(dp):
-            proj_out[k, i : i + 1, :] = window[k : k + 1, :]
-
-    fifth_copies = [None] * dp
-    for k in range(1, dp):
-        fifth_copies[k] = send(
-            proj_out.at[k], proj_in.at[me], s5.at[k], r5.at[k], {"dp": plane_source(plane[k])}
-        )
-    proj_in[me] = proj_out[0]
-    for k in range(1, dp):
-        fifth_copies[k].wait_recv()
+        att_in[...].reshape(side * rows, q_cols), oweight[...], contract_last, preferred_element_type=F32
+    ).astype(BF16)
+
+    for k in range(side):
+        for t in range(tensor):
+            first = k * rows + t * mine
+            red_out[k, t] = products[first : first + mine, :]
+    fourth_copies = []
+    for k in reversed(range(side)):
+        for step in reversed(range(tensor)):
+            if k or step:
+                peer_t = line_peer(line[step])
+                fourth_copies.append(
+                    send(
+                        red_out.at[k, peer_t], red_in.at[my_x, step], s4.at[k, step], r4.at[k, step],
+                        {"dp": plane_source((ring[k], 0)), "tensor": peer_t},
+                    )
+                )
+    red_in[my_x, 0] = red_out[0, me_t]
+    for copy in fourth_copies:
+        copy.wait_recv()
     tiles = [jnp.zeros((mine, LANES), F32) for _ in range(width // LANES)]
-    for d in range(dp):
-        first = share * d
-        low = first // LANES
-        for c in range((first + share - 1) // LANES - low + 1):
-            tiles[low + c] = tiles[low + c] + proj_in[d, :, c * LANES : (c + 1) * LANES]
+    for column in range(side):
+        low = column * side * share // LANES
+        for c in range(strip // LANES):
+            if low + c < len(tiles):
+                for step in range(tensor):
+                    tiles[low + c] = tiles[low + c] + red_in[column, step, :, c * LANES : (c + 1) * LANES].astype(F32)
     square = tiles[0] * tiles[0]
     for tile in tiles[1:]:
         square = square + tile * tile
@@ -334,16 +351,21 @@
 
     keep = pltpu.make_async_copy(row_out, hid_hbm.at[me_t], last_sem)
     keep.start()
-    sixth_copies = [None] * tensor
-    for k in range(1, tensor):
-        sixth_copies[k] = send(
-            row_out, hid_hbm.at[me_t], s6.at[k], r6.at[k], {"tensor": line_peer(line[k])}
-        )
-    for k in range(1, tensor):
-        sixth_copies[k].wait_recv()
+    fifth_copies = [
+        send(row_out, hid_hbm.at[me_t], s5.at[k], r5.at[k], {"tensor": line_peer(line[k])})
+        for k in reversed(range(1, tensor))
+    ]
+    for copy in fifth_copies:
+        copy.wait_recv()
     keep.wait()
     for copy in sends:
         copy.wait_send()
+
+
+def finish_kernel(hid_in, nk_in, nv_in, hid, nk, nv):
+    hid[...] = hid_in[...].reshape(hid.shape)
+    nk[...] = nk_in[...]
+    nv[...] = nv_in[...]
 
 
 def per_device(dp, tensor, side, *args):
@@ -355,7 +377,8 @@
     share_pad = padded(share)
     cols = q_cols + 2 * kv_cols
     mine = rows // tensor
-    dims = (dp, tensor, side, rows, width, share, q_cols, kv_cols, ctx)
+    strip = padded(side * share + max(side * share * a % LANES for a in range(side)))
+    dims = (dp, tensor, side, rows, width, share, q_cols, kv_cols, ctx, strip)
     exponent = np.arange(HD // 2, dtype=np.float64) * (2.0 / HD)
     frequency = (ROPE_BASE**-exponent).astype(np.float32)
     freq = jnp.asarray(np.concatenate([frequency, frequency])[None])
@@ -381,7 +404,7 @@
             pltpu.VMEM((1, HD), F32),
             pltpu.VMEM((rows, ctx, kv_cols), BF16),
             pltpu.VMEM((rows, ctx, kv_cols), BF16),
-            pltpu.VMEM((share, q_cols), BF16),
+            pltpu.VMEM((strip, q_cols), BF16),
             pltpu.VMEM((1, width), F32),
             pltpu.VMEM((1, HD), F32),
             pltpu.VMEM((rows, width + 2 * LANES), F32),
@@ -392,29 +415,39 @@
             pltpu.VMEM((dp, rows, cols), BF16),
             pltpu.VMEM((ctx // 2, HD), F32),
             pltpu.VMEM((HD, ctx // 2), BF16),
-            pltpu.VMEM((dp, rows, q_cols), BF16),
-            pltpu.VMEM((share_pad // LANES, dp * rows, LANES), F32),
-            pltpu.VMEM((tensor, mine, dp, share_pad), BF16),
-            pltpu.VMEM((tensor, mine, dp, share_pad), BF16),
-            pltpu.VMEM((dp, mine, share_pad + LANES), F32),
-            pltpu.VMEM((dp, mine, share_pad + LANES), F32),
+            pltpu.VMEM((side, rows, q_cols), BF16),
+            pltpu.VMEM((side, tensor, mine, strip), BF16),
+            pltpu.VMEM((side, tensor, mine, strip), BF16),
             pltpu.VMEM((mine, width), BF16),
             dma((12,)),
             dma((2, rows)),
             dma((dp,)), dma((dp,)),
             dma((dp,)), dma((dp,)),
-            dma((dp,)), dma((dp,)),
+            dma((side,)), dma((side,)),
+            dma((side, tensor)), dma((side, tensor)),
             dma((tensor,)), dma((tensor,)),
-            dma((dp,)), dma((dp,)),
-            dma((tensor,)), dma((tensor,)),
+            dma((2, 3)), dma((2, 3)),
             dma(()),
         ],
-        compiler_params=pltpu.CompilerParams(collective_id=0, has_side_effects=True),
+        compiler_params=pltpu.CompilerParams(collective_id=0, has_side_effects=True, vmem_limit_bytes=50 * 1024 * 1024),
     )(
-        tokens, lengths.reshape(1, rows), positions.reshape(1, rows), in_gain.reshape(1, width), qw, kw, vw,
-        q_gain.reshape(1, HD), k_gain.reshape(1, HD), kc, vc, ow.T, post_gain.reshape(1, width), freq,
+        *[
+            pltpu.with_memory_space_constraint(operand, pltpu.HBM)
+            for operand in (
+                tokens, lengths.reshape(1, rows), positions.reshape(1, rows), in_gain, qw, kw, vw,
+                q_gain.reshape(1, HD), k_gain.reshape(1, HD), kc, vc, ow.T, post_gain, freq,
+            )
+        ]
     )
-    return hidden.reshape(rows, width), new_keys, new_values
+    return pl.pallas_call(
+        finish_kernel,
+        out_shape=(
+            jax.ShapeDtypeStruct((rows, width), BF16),
+            jax.ShapeDtypeStruct((rows, kv_cols), BF16),
+            jax.ShapeDtypeStruct((rows, kv_cols), BF16),
+        ),
+        compiler_params=pltpu.CompilerParams(vmem_limit_bytes=4 * 1024 * 1024),
+    )(hidden, new_keys, new_values)
 
 
 def solution(mesh):

time: 57.5 us -> 46.7 us (0.81)
  local copies, waits for them, and re-layouts: 6.96 us -> 0 us
  Pallas kernels: 49.5 us -> 45.9 us
    reshape x3 -> x0, local copies, waits for them, and re-layouts: 4.37 us -> none  [the longest x1 1.65 us: per_device(): return (hidden.reshape(rows, width), new_keys, new_values)]
    pallas_call x1, Pallas kernels: 49.5 us -> 45.2 us  [per_device(): pl.pallas_call(functools.partial(kernel, dims), out_shape=(jax.ShapeDtype...]
    unnamed x2 -> x0, local copies, waits for them, and re-layouts: 2.59 us -> none
    pallas_call x0 -> x1, Pallas kernels: none -> 0.7 us  [per_device(): pl.pallas_call(finish_kernel, out_shape=(jax.ShapeDtypeStruct((rows, widt...]
where the time goes in v2:
time: 46.7 us; the launch traced here: 46.6 us
  Pallas kernels  45.9 us (98%)
  between operations  0.64 us (1%)
    pallas_call x1, Pallas kernels, per_device(): pl.pallas_call(functools.partial(kernel, dims), out_shape=(jax.ShapeDtype...  45.2 us

profile of v2, /device:TPU:1, one launch (start us, length us, event | category | flops | bytes accessed | tf_op | source)
XLA Modules:
  0.0 46.6 jit_solution(5935323755900152918)
XLA Ops:
  0.6 45.2 %shard_map.157 = (bf16[8,2,5376]{2,1,0:T(2,128)(2,1)S(1)}, bf16[16,256]{1,0:T(8,128)(2,1)S(1)}, bf16[16,256]{1,0:T(8,128)(2,1)S(1)}) custom-call(bf16[16,5376]{1,0:T(8,128)(2,1)} %tokens_hbm.1, s32[1,16]{1,0:T(1,128)} %bitcast.6, s32[1,16]{1,0:T(1,128)} %bitcast.7, f32[5376]{0:T(1024)} %in_gain_hbm.1, bf16[336,512]{1,0:T(8,128)(2,1)} %qw_hbm.1, ...), custom_call_target="tpu_custom_call" | custom-call | tf_op jit(solution)/shard_map/pallas_call | solution.py:388
  45.9 0.7 %shard_map.158 = (bf16[16,5376]{1,0:T(8,128)(2,1)}, bf16[16,256]{1,0:T(8,128)(2,1)}, bf16[16,256]{1,0:T(8,128)(2,1)}) custom-call(bf16[8,2,5376]{2,1,0:T(2,128)(2,1)S(1)} %get-tuple-element.6.hid_in, bf16[16,256]{1,0:T(8,128)(2,1)S(1)} %get-tuple-element.7.nk_in, bf16[16,256]{1,0:T(8,128)(2,1)S(1)} %get-tuple-element.8.nv_in), custom_call_target="tpu_custom_call" | custom-call | tf_op jit(solution)/shard_map/pallas_call | solution.py:442

commit v3 on v2

--- a/solution.py
+++ b/solution.py
@@ -43,7 +43,7 @@
     kc_hbm, vc_hbm, ow_hbm, post_gain_hbm, freq_hbm,
     hid_hbm, nk_out, nv_out,
     tokens, lengths, positions, in_gain, weights, q_gain, k_gain, kcache, vcache, oweight, post_gain, freq,
-    normed, tok_mine, slots, spread, part_out, part_in, scores, probs, att_in, red_out, red_in, row_out,
+    normed, tok_mine, slots, spread, part_out, part_in, other_out, other_in, scores, probs, att_in, red_out, red_in, row_out,
     load_sem, cache_sem, s1, r1, s2, r2, s3, r3, s4, r4, s5, r5, sw, rw, last_sem,
 ):
     dp, tensor, side, rows, width, share, q_cols, kv_cols, ctx, strip = dims
@@ -68,6 +68,18 @@
     def plane_source(step):
         return xs[-step[0]] * side + ys[-step[1]]
 
+    first_core = my_c == 0
+    place = jnp.where(first_core, my_x, my_y)
+    across = jnp.where(first_core, my_y, my_x)
+    along_x = [xs[a] * side + my_y for a in range(side)]
+    along_y = [my_x * side + ys[a] for a in range(side)]
+
+    def gather_peer(a):
+        return jnp.where(first_core, along_y[a], along_x[a])
+
+    def spread_peer(a):
+        return jnp.where(first_core, along_x[a], along_y[a])
+
     def line_peer(step):
         return zs[step[0]] * 2 + cs[step[1]]
 
@@ -75,21 +87,21 @@
     line = line_offsets(depth)
     ring = sorted(range(side), key=lambda a: (ring_distance(a, side), a))
 
-    skew = lax.rem(my_x * (side * share), LANES)
-    edge = strip - side * share
-    oweight[:edge, :] = jnp.zeros((edge, q_cols), BF16)
-    oweight[side * share :, :] = jnp.zeros((edge, q_cols), BF16)
+    for a in range(side):
+        oweight[a * share_pad + share : (a + 1) * share_pad, :] = jnp.zeros((share_pad - share, q_cols), BF16)
 
     barrier = pltpu.get_barrier_semaphore()
-    for step in reversed(plane[1:]):
-        pl.semaphore_signal(barrier, inc=1, device_id={"dp": plane_peer(step)}, device_id_type=MESH)
-    for kx, ahead in enumerate(ring):
-        for kt, step in enumerate(line):
-            if kt:
-                pl.semaphore_signal(
-                    barrier, inc=1, device_id={"dp": plane_peer((ahead, 0)), "tensor": line_peer(step)},
-                    device_id_type=MESH,
-                )
+    greeted = [({"dp": plane_peer(step)}) for step in reversed(plane[1:])]
+    for step in reversed(line[1:]):
+        greeted.append({"tensor": line_peer(step)})
+        for a in range(1, side):
+            if step[1]:
+                greeted.append({"dp": along_x[a], "tensor": line_peer(step)})
+                greeted.append({"dp": along_y[a], "tensor": line_peer(step)})
+            else:
+                greeted.append({"dp": spread_peer(a), "tensor": line_peer(step)})
+    for device in greeted:
+        pl.semaphore_signal(barrier, inc=1, device_id=device, device_id_type=MESH)
 
     def load(src, dst, at):
         copy = pltpu.make_async_copy(src, dst, load_sem.at[at])
@@ -107,10 +119,10 @@
         load(lengths_hbm, lengths, 5), load(positions_hbm, positions, 6), load(q_gain_hbm, q_gain, 7),
         load(k_gain_hbm, k_gain, 8), load(post_gain_hbm, post_gain.at[0], 9), load(freq_hbm, freq, 10),
     ]
-    def rows_of(y, first, count):
-        return oweight.at[pl.ds(pl.multiple_of(skew + y * share + first, 16), count), :]
-
-    own_block = rows_of(my_y, 0, share)
+    def rows_of(at, first, count):
+        return oweight.at[pl.ds(pl.multiple_of(at * share_pad + first, 16), count), :]
+
+    own_block = rows_of(across, 0, share)
     c_ow = load(ow_hbm, own_block, 11)
 
     c_tokens.wait()
@@ -127,7 +139,7 @@
             window = pltpu.roll(window, window.shape[1] - (first - low), 1)
         slots[d] = window[:, :share_pad].astype(BF16)
 
-    pl.semaphore_wait(barrier, dp - 1 + side * (tensor - 1))
+    pl.semaphore_wait(barrier, len(greeted))
 
     sends = []
 
@@ -144,13 +156,13 @@
         peer = plane_peer(plane[k])
         first_copies[k] = send(slots.at[peer], spread.at[k], s1.at[k], r1.at[k], {"dp": peer})
     spread[0] = slots[me]
-    early = -(-share // 32) * 16
-    ways = ((1, 0, early), (side - 1, share - early, 0))
+    far = -(-share // 32) * 16
     c_ow.wait()
+    ways = ((1, 0, far), (side - 1, far, share - far))
     early_copies = []
-    for way, (step, first, _) in enumerate(ways):
-        piece = rows_of(my_y, first, early)
-        early_copies.append(send(piece, piece, sw.at[way, 0], rw.at[way, 0], {"dp": plane_peer((0, step))}))
+    for way, (step, first, count) in enumerate(ways):
+        piece = rows_of(across, first, count)
+        early_copies.append(send(piece, piece, sw.at[way, 0], rw.at[way, 0], {"dp": gather_peer(step)}))
 
     c_k, c_v = [], []
     for b in range(rows):
@@ -186,7 +198,7 @@
 
     group = max(dp // 4, 1)
     own_part = None
-    second_copies = [None] * dp
+    second_copies, other_copies = [None] * dp, [None] * dp
     for g0 in range(0, dp, group):
         for k in range(max(g0, 1), g0 + group):
             first_copies[k].wait_recv()
@@ -194,25 +206,31 @@
         part = jnp.dot(lhs, weights[...], preferred_element_type=F32)
         if g0 == 0:
             own_part = part[:rows]
-        part_out[g0 : g0 + group] = part.astype(BF16).reshape(group, rows, part.shape[1])
+        sent = part.astype(BF16).reshape(group, rows, part.shape[1])
+        part_out[g0 : g0 + group] = sent[:, :, :q_cols]
+        other_out[g0 : g0 + group] = sent[:, :, q_cols:]
         for k in range(max(g0, 1), g0 + group):
             second_copies[k] = send(
-                part_out.at[k], part_in.at[k], s2.at[k], r2.at[k], {"dp": plane_source(plane[k])}
+                part_out.at[k], part_in.at[k], s2.at[0, k], r2.at[0, k], {"dp": plane_source(plane[k])}
             )
-
-    joined = own_part
+    for k in range(1, dp):
+        other_copies[k] = send(
+            other_out.at[k], other_in.at[k], s2.at[1, k], r2.at[1, k], {"dp": plane_source(plane[k])}
+        )
+
+    joined = own_part[:, :q_cols]
     for k in range(1, dp):
         second_copies[k].wait_recv()
         joined = joined + part_in[k].astype(F32)
 
-    late_copies = []
     for copy in early_copies:
         copy.wait_recv()
-    for way, (step, first, rest) in enumerate(ways):
-        piece = rows_of(ys[-step], way * early, early if way == 0 else share - early)
-        late_copies.append(send(piece, piece, sw.at[way, 1], rw.at[way, 1], {"dp": plane_peer((0, step))}))
-        piece = rows_of(my_y, rest, share - early)
-        late_copies.append(send(piece, piece, sw.at[way, 2], rw.at[way, 2], {"dp": plane_peer((0, step))}))
+    late_copies = []
+    for way, (step, first, count) in enumerate(ways):
+        piece = rows_of(jnp.where(first_core, ys[-step], xs[-step]), first, count)
+        late_copies.append(send(piece, piece, sw.at[way, 1], rw.at[way, 1], {"dp": gather_peer(step)}))
+        piece = rows_of(across, *ways[1 - way][1:])
+        late_copies.append(send(piece, piece, sw.at[way, 2], rw.at[way, 2], {"dp": gather_peer(step)}))
 
     def rms_rope(vectors, gain):
         square = jnp.sum(vectors * vectors, axis=1, keepdims=True) * (1.0 / HD)
@@ -222,13 +240,6 @@
     queries = [
         (rms_rope(joined[:, h * HD : (h + 1) * HD], q_gain[...]) * QPRE ** (-0.5)).astype(BF16) for h in range(heads)
     ]
-    new_keys = jnp.concatenate(
-        [rms_rope(joined[:, q_cols + g * HD : q_cols + (g + 1) * HD], k_gain[...]) for g in range(kv_heads)], axis=1
-    ).astype(BF16)
-    new_values = joined[:, q_cols + kv_cols :].astype(BF16)
-    nk_out[...] = new_keys
-    nv_out[...] = new_values
-
     zero_head = jnp.zeros((rows, HD), BF16)
     stacked = [
         jnp.concatenate([queries[h] if g == h // per_kv else zero_head for g in range(kv_heads)], axis=1)
@@ -272,6 +283,17 @@
         scores[m * block_rows : (m + 1) * block_rows, :] = total
         top = jnp.max(total, axis=0, keepdims=True)
         largest = top if largest is None else jnp.maximum(largest, top)
+    others = own_part[:, q_cols:]
+    for k in range(1, dp):
+        other_copies[k].wait_recv()
+        others = others + other_in[k].astype(F32)
+    new_keys = jnp.concatenate(
+        [rms_rope(others[:, g * HD : (g + 1) * HD], k_gain[...]) for g in range(kv_heads)], axis=1
+    ).astype(BF16)
+    new_values = others[:, kv_cols:].astype(BF16)
+    nk_out[...] = new_keys
+    nv_out[...] = new_values
+
     own_scores = lax.dot_general(
         new_keys, jnp.concatenate([query_rows, query_rows], axis=0), contract_last, preferred_element_type=F32
     )
@@ -307,7 +329,7 @@
     third_copies = [None] * side
     for k in reversed(range(1, side)):
         third_copies[k] = send(
-            att_in.at[0], att_in.at[k], s3.at[k], r3.at[k], {"dp": plane_peer((ring[k], 0))}
+            att_in.at[0], att_in.at[k], s3.at[k], r3.at[k], {"dp": spread_peer(ring[k])}
         )
     for copy in late_copies:
         copy.wait_recv()
@@ -323,25 +345,40 @@
             red_out[k, t] = products[first : first + mine, :]
     fourth_copies = []
     for k in reversed(range(side)):
-        for step in reversed(range(tensor)):
-            if k or step:
-                peer_t = line_peer(line[step])
+        for turn, (step_z, step_c) in reversed(list(enumerate(line))):
+            if k or turn:
+                peer_t = line_peer((step_z, step_c))
+                slot = red_in.at[my_c, place, step_z]
                 fourth_copies.append(
                     send(
-                        red_out.at[k, peer_t], red_in.at[my_x, step], s4.at[k, step], r4.at[k, step],
-                        {"dp": plane_source((ring[k], 0)), "tensor": peer_t},
+                        red_out.at[k, peer_t], slot, s4.at[k, turn], r4.at[k, turn],
+                        {"dp": spread_peer(-ring[k] % side), "tensor": peer_t},
                     )
                 )
-    red_in[my_x, 0] = red_out[0, me_t]
+    red_in[my_c, place, 0] = red_out[0, me_t]
     for copy in fourth_copies:
         copy.wait_recv()
     tiles = [jnp.zeros((mine, LANES), F32) for _ in range(width // LANES)]
-    for column in range(side):
-        low = column * side * share // LANES
-        for c in range(strip // LANES):
-            if low + c < len(tiles):
-                for step in range(tensor):
-                    tiles[low + c] = tiles[low + c] + red_in[column, step, :, c * LANES : (c + 1) * LANES].astype(F32)
+    lane_pair = lax.broadcasted_iota(jnp.int32, (mine, LANES), 1)
+    for d in range(dp):
+        parts = []
+        for c, p, a in ((0, d // side, d % side), (1, d % side, d // side)):
+            for z in range(depth):
+                parts.append(red_in[c, p, z, :, a * share_pad : (a + 1) * share_pad].astype(F32))
+        while len(parts) > 1:
+            parts = [parts[n] + parts[n + 1] for n in range(0, len(parts) - 1, 2)] + parts[len(parts) // 2 * 2 :]
+        low, turn = share * d // LANES, share * d % LANES
+        columns = [parts[0][:, n * LANES : (n + 1) * LANES] for n in range(share_pad // LANES)]
+        if turn:
+            columns = [pltpu.roll(column, turn, 1) for column in columns]
+            none = jnp.zeros((mine, LANES), F32)
+            columns = [
+                jnp.where(lane_pair < turn, before, after)
+                for before, after in zip([none] + columns, columns + [none])
+            ]
+        for n, column in enumerate(columns):
+            if low + n < len(tiles) and n * LANES < turn + share:
+                tiles[low + n] = tiles[low + n] + column
     square = tiles[0] * tiles[0]
     for tile in tiles[1:]:
         square = square + tile * tile
@@ -355,11 +392,11 @@
         send(row_out, hid_hbm.at[me_t], s5.at[k], r5.at[k], {"tensor": line_peer(line[k])})
         for k in reversed(range(1, tensor))
     ]
+    for copy in sends:
+        copy.wait_send()
+    keep.wait()
     for copy in fifth_copies:
         copy.wait_recv()
-    keep.wait()
-    for copy in sends:
-        copy.wait_send()
 
 
 def finish_kernel(hid_in, nk_in, nv_in, hid, nk, nv):
@@ -377,7 +414,8 @@
     share_pad = padded(share)
     cols = q_cols + 2 * kv_cols
     mine = rows // tensor
-    strip = padded(side * share + max(side * share * a % LANES for a in range(side)))
+    depth = tensor // 2
+    strip = side * share_pad
     dims = (dp, tensor, side, rows, width, share, q_cols, kv_cols, ctx, strip)
     exponent = np.arange(HD // 2, dtype=np.float64) * (2.0 / HD)
     frequency = (ROPE_BASE**-exponent).astype(np.float32)
@@ -411,18 +449,20 @@
             pltpu.VMEM((mine, width), F32),
             pltpu.VMEM((dp, rows, share_pad), BF16),
             pltpu.VMEM((dp, rows, share_pad), BF16),
-            pltpu.VMEM((dp, rows, cols), BF16),
-            pltpu.VMEM((dp, rows, cols), BF16),
+            pltpu.VMEM((dp, rows, q_cols), BF16),
+            pltpu.VMEM((dp, rows, q_cols), BF16),
+            pltpu.VMEM((dp, rows, 2 * kv_cols), BF16),
+            pltpu.VMEM((dp, rows, 2 * kv_cols), BF16),
             pltpu.VMEM((ctx // 2, HD), F32),
             pltpu.VMEM((HD, ctx // 2), BF16),
             pltpu.VMEM((side, rows, q_cols), BF16),
             pltpu.VMEM((side, tensor, mine, strip), BF16),
-            pltpu.VMEM((side, tensor, mine, strip), BF16),
+            pltpu.VMEM((2, side, depth, mine, strip), BF16),
             pltpu.VMEM((mine, width), BF16),
             dma((12,)),
             dma((2, rows)),
             dma((dp,)), dma((dp,)),
-            dma((dp,)), dma((dp,)),
+            dma((2, dp)), dma((2, dp)),
             dma((side,)), dma((side,)),
             dma((side, tensor)), dma((side, tensor)),
             dma((tensor,)), dma((tensor,)),

time: 46.7 us -> 44.9 us (0.961)
  Pallas kernels: 45.9 us -> 44.2 us
    pallas_call x1, Pallas kernels: 45.2 us -> 43.5 us  [per_device(): pl.pallas_call(functools.partial(kernel, dims), out_shape=(jax.ShapeDtype...]
where the time goes in v3:
time: 44.9 us; the launch traced here: 44.8 us
  Pallas kernels  44.2 us (98%)
  between operations  0.64 us (1%)
    pallas_call x1, Pallas kernels, per_device(): pl.pallas_call(functools.partial(kernel, dims), out_shape=(jax.ShapeDtype...  43.5 us

profile of v3, /device:TPU:1, one launch (start us, length us, event | category | flops | bytes accessed | tf_op | source)
XLA Modules:
  0.0 44.8 jit_solution(12449186744854575778)
XLA Ops:
  0.6 43.5 %shard_map.157 = (bf16[8,2,5376]{2,1,0:T(2,128)(2,1)S(1)}, bf16[16,256]{1,0:T(8,128)(2,1)S(1)}, bf16[16,256]{1,0:T(8,128)(2,1)S(1)}) custom-call(bf16[16,5376]{1,0:T(8,128)(2,1)} %tokens_hbm.1, s32[1,16]{1,0:T(1,128)} %bitcast.6, s32[1,16]{1,0:T(1,128)} %bitcast.7, f32[5376]{0:T(1024)} %in_gain_hbm.1, bf16[336,512]{1,0:T(8,128)(2,1)} %qw_hbm.1, ...), custom_call_target="tpu_custom_call" | custom-call | tf_op jit(solution)/shard_map/pallas_call | solution.py:426
  44.1 0.7 %shard_map.158 = (bf16[16,5376]{1,0:T(8,128)(2,1)}, bf16[16,256]{1,0:T(8,128)(2,1)}, bf16[16,256]{1,0:T(8,128)(2,1)}) custom-call(bf16[8,2,5376]{2,1,0:T(2,128)(2,1)S(1)} %get-tuple-element.6.hid_in, bf16[16,256]{1,0:T(8,128)(2,1)S(1)} %get-tuple-element.7.nk_in, bf16[16,256]{1,0:T(8,128)(2,1)S(1)} %get-tuple-element.8.nv_in), custom_call_target="tpu_custom_call" | custom-call | tf_op jit(solution)/shard_map/pallas_call | solution.py:482

commit v4 on v3

--- a/solution.py
+++ b/solution.py
@@ -152,7 +152,7 @@
         return copy
 
     first_copies = [None] * dp
-    for k in range(1, dp):
+    for k in reversed(range(1, dp)):
         peer = plane_peer(plane[k])
         first_copies[k] = send(slots.at[peer], spread.at[k], s1.at[k], r1.at[k], {"dp": peer})
     spread[0] = slots[me]
@@ -196,10 +196,17 @@
     for copy in c_w:
         copy.wait()
 
-    group = max(dp // 4, 1)
+    group = max(dp // 2, 1)
     own_part = None
-    second_copies, other_copies = [None] * dp, [None] * dp
-    for g0 in range(0, dp, group):
+    part_rows = rows // 2
+    second_copies, other_copies = [[None] * dp for _ in range(2)], [None] * dp
+
+    def send_part(n, k):
+        second_copies[n][k] = send(
+            part_out.at[n, k], part_in.at[n, k], s2.at[n, k], r2.at[n, k], {"dp": plane_source(plane[k])}
+        )
+
+    for g0 in reversed(range(0, dp, group)):
         for k in range(max(g0, 1), g0 + group):
             first_copies[k].wait_recv()
         lhs = spread[g0 : g0 + group].reshape(group * rows, share_pad)
@@ -207,48 +214,46 @@
         if g0 == 0:
             own_part = part[:rows]
         sent = part.astype(BF16).reshape(group, rows, part.shape[1])
-        part_out[g0 : g0 + group] = sent[:, :, :q_cols]
         other_out[g0 : g0 + group] = sent[:, :, q_cols:]
-        for k in range(max(g0, 1), g0 + group):
-            second_copies[k] = send(
-                part_out.at[k], part_in.at[k], s2.at[0, k], r2.at[0, k], {"dp": plane_source(plane[k])}
-            )
-    for k in range(1, dp):
+        for k in reversed(range(max(g0, 1), g0 + group)):
+            for n in range(2):
+                first = (k - g0) * rows + n * part_rows
+                part_out[n, k] = part[first : first + part_rows, :q_cols].astype(BF16)
+        for k in reversed(range(max(g0, 1), g0 + group)):
+            send_part(0, k)
+    for k in reversed(range(1, dp)):
+        send_part(1, k)
+    for k in reversed(range(1, dp)):
         other_copies[k] = send(
-            other_out.at[k], other_in.at[k], s2.at[1, k], r2.at[1, k], {"dp": plane_source(plane[k])}
+            other_out.at[k], other_in.at[k], s2.at[2, k], r2.at[2, k], {"dp": plane_source(plane[k])}
         )
 
-    joined = own_part[:, :q_cols]
-    for k in range(1, dp):
-        second_copies[k].wait_recv()
-        joined = joined + part_in[k].astype(F32)
-
-    for copy in early_copies:
-        copy.wait_recv()
-    late_copies = []
-    for way, (step, first, count) in enumerate(ways):
-        piece = rows_of(jnp.where(first_core, ys[-step], xs[-step]), first, count)
-        late_copies.append(send(piece, piece, sw.at[way, 1], rw.at[way, 1], {"dp": gather_peer(step)}))
-        piece = rows_of(across, *ways[1 - way][1:])
-        late_copies.append(send(piece, piece, sw.at[way, 2], rw.at[way, 2], {"dp": gather_peer(step)}))
-
-    def rms_rope(vectors, gain):
+    def rms_rope(vectors, gain, first):
+        count = vectors.shape[0]
         square = jnp.sum(vectors * vectors, axis=1, keepdims=True) * (1.0 / HD)
         scaled = vectors * lax.rsqrt(square + EPS) * gain
-        return scaled * cos_part + pltpu.roll(scaled, HD // 2, 1) * sin_part
-
-    queries = [
-        (rms_rope(joined[:, h * HD : (h + 1) * HD], q_gain[...]) * QPRE ** (-0.5)).astype(BF16) for h in range(heads)
-    ]
-    zero_head = jnp.zeros((rows, HD), BF16)
-    stacked = [
-        jnp.concatenate([queries[h] if g == h // per_kv else zero_head for g in range(kv_heads)], axis=1)
-        for h in range(heads)
-    ]
-    used = heads * rows
-    if used < HD // 2:
-        stacked.append(jnp.zeros((HD // 2 - used, kv_cols), BF16))
-    query_rows = jnp.concatenate(stacked, axis=0)
+        return (
+            scaled * cos_part[first : first + count]
+            + pltpu.roll(scaled, HD // 2, 1) * sin_part[first : first + count]
+        )
+
+    def queries_of(n):
+        first = n * part_rows
+        joined = own_part[first : first + part_rows, :q_cols]
+        for k in range(1, dp):
+            second_copies[n][k].wait_recv()
+            joined = joined + part_in[n, k].astype(F32)
+        zeros_part = jnp.zeros((part_rows, HD), F32)
+        stacked = []
+        for h in range(heads):
+            query = rms_rope(joined[:, h * HD : (h + 1) * HD], q_gain[...], first) * QPRE ** (-0.5)
+            both = jnp.concatenate([zeros_part, query] if n else [query, zeros_part], axis=0)
+            nothing = jnp.zeros((rows, HD), F32)
+            stacked.append(jnp.concatenate([both if g == h // per_kv else nothing for g in range(kv_heads)], axis=1))
+        if heads * rows < HD // 2:
+            stacked.append(jnp.zeros((HD // 2 - heads * rows, kv_cols), F32))
+        return jnp.concatenate(stacked, axis=0).astype(BF16)
+
     half_rows = HD // 2
     query_of = lax.broadcasted_iota(jnp.int32, (half_rows, 1), 0) % rows
     zeros_half = jnp.zeros((half_rows, kv_cols), BF16)
@@ -259,26 +264,41 @@
     slots_half = ctx // 2
     block_rows = min(256, slots_half)
     blocks = slots_half // block_rows
-    low_q, high_q = [], []
-    for b in range(rows):
-        only = query_rows * picks[b]
-        low_q.append(jnp.concatenate([only, zeros_half], axis=0))
-        high_q.append(jnp.concatenate([zeros_half, only], axis=0))
     lane_row = lax.broadcasted_iota(jnp.int32, (1, HD), 1)
     base_slot = jnp.where(lane_row < half_rows, 0, slots_half)
+
+    def scores_of(query_part, n, m):
+        total = None
+        for b in range(n * part_rows, (n + 1) * part_rows):
+            only = query_part * picks[b]
+            for high in range(2):
+                first = high * slots_half + m * block_rows
+                one = lax.dot_general(
+                    kcache[b, first : first + block_rows, :],
+                    jnp.concatenate([zeros_half, only] if high else [only, zeros_half], axis=0),
+                    contract_last, preferred_element_type=F32,
+                )
+                total = one if total is None else total + one
+        return total
+
+    query_parts = [queries_of(0)]
+    for copy in early_copies:
+        copy.wait_recv()
+    late_copies = []
+    for way, (step, first, count) in enumerate(ways):
+        piece = rows_of(jnp.where(first_core, ys[-step], xs[-step]), first, count)
+        late_copies.append(send(piece, piece, sw.at[way, 1], rw.at[way, 1], {"dp": gather_peer(step)}))
+        piece = rows_of(across, *ways[1 - way][1:])
+        late_copies.append(send(piece, piece, sw.at[way, 2], rw.at[way, 2], {"dp": gather_peer(step)}))
+
+    for m in range(blocks):
+        scores[m * block_rows : (m + 1) * block_rows, :] = scores_of(query_parts[0], 0, m)
+    query_parts.append(queries_of(1))
+    query_rows = query_parts[0] + query_parts[1]
     largest = None
     for m in range(blocks):
-        total = None
-        for b in range(rows):
-            low = lax.dot_general(
-                kcache[b, m * block_rows : (m + 1) * block_rows, :], low_q[b], contract_last, preferred_element_type=F32
-            )
-            high = lax.dot_general(
-                kcache[b, slots_half + m * block_rows : slots_half + (m + 1) * block_rows, :], high_q[b],
-                contract_last, preferred_element_type=F32,
-            )
-            total = low + high if total is None else total + low + high
         slot = lax.broadcasted_iota(jnp.int32, (block_rows, HD), 0) + (m * block_rows) + base_slot
+        total = scores[m * block_rows : (m + 1) * block_rows, :] + scores_of(query_parts[1], 1, m)
         total = jnp.where(slot < len_row, total, -jnp.inf)
         scores[m * block_rows : (m + 1) * block_rows, :] = total
         top = jnp.max(total, axis=0, keepdims=True)
@@ -288,7 +308,7 @@
         other_copies[k].wait_recv()
         others = others + other_in[k].astype(F32)
     new_keys = jnp.concatenate(
-        [rms_rope(others[:, g * HD : (g + 1) * HD], k_gain[...]) for g in range(kv_heads)], axis=1
+        [rms_rope(others[:, g * HD : (g + 1) * HD], k_gain[...], 0) for g in range(kv_heads)], axis=1
     ).astype(BF16)
     new_values = others[:, kv_cols:].astype(BF16)
     nk_out[...] = new_keys
@@ -449,8 +469,8 @@
             pltpu.VMEM((mine, width), F32),
             pltpu.VMEM((dp, rows, share_pad), BF16),
             pltpu.VMEM((dp, rows, share_pad), BF16),
-            pltpu.VMEM((dp, rows, q_cols), BF16),
-            pltpu.VMEM((dp, rows, q_cols), BF16),
+            pltpu.VMEM((2, dp, rows // 2, q_cols), BF16),
+            pltpu.VMEM((2, dp, rows // 2, q_cols), BF16),
             pltpu.VMEM((dp, rows, 2 * kv_cols), BF16),
             pltpu.VMEM((dp, rows, 2 * kv_cols), BF16),
             pltpu.VMEM((ctx // 2, HD), F32),
@@ -462,7 +482,7 @@
             dma((12,)),
             dma((2, rows)),
             dma((dp,)), dma((dp,)),
-            dma((2, dp)), dma((2, dp)),
+            dma((3, dp)), dma((3, dp)),
             dma((side,)), dma((side,)),
             dma((side, tensor)), dma((side, tensor)),
             dma((tensor,)), dma((tensor,)),

time: 44.9 us -> 44.2 us (0.984)
  Pallas kernels: 44.2 us -> 43.4 us
    pallas_call x1, Pallas kernels: 43.5 us -> 42.7 us  [per_device(): pl.pallas_call(functools.partial(kernel, dims), out_shape=(jax.ShapeDtype...]
where the time goes in v4:
time: 44.2 us; the launch traced here: 44.1 us
  Pallas kernels  43.4 us (98%)
  between operations  0.64 us (1%)
    pallas_call x1, Pallas kernels, per_device(): pl.pallas_call(functools.partial(kernel, dims), out_shape=(jax.ShapeDtype...  42.7 us

profile of v4, /device:TPU:1, one launch (start us, length us, event | category | flops | bytes accessed | tf_op | source)
XLA Modules:
  0.0 44.1 jit_solution(478720041998389042)
XLA Ops:
  0.6 42.7 %shard_map.157 = (bf16[8,2,5376]{2,1,0:T(2,128)(2,1)S(1)}, bf16[16,256]{1,0:T(8,128)(2,1)S(1)}, bf16[16,256]{1,0:T(8,128)(2,1)S(1)}) custom-call(bf16[16,5376]{1,0:T(8,128)(2,1)} %tokens_hbm.1, s32[1,16]{1,0:T(1,128)} %bitcast.6, s32[1,16]{1,0:T(1,128)} %bitcast.7, f32[5376]{0:T(1024)} %in_gain_hbm.1, bf16[336,512]{1,0:T(8,128)(2,1)} %qw_hbm.1, ...), custom_call_target="tpu_custom_call" | custom-call | tf_op jit(solution)/shard_map/pallas_call | solution.py:446
  43.4 0.7 %shard_map.158 = (bf16[16,5376]{1,0:T(8,128)(2,1)}, bf16[16,256]{1,0:T(8,128)(2,1)}, bf16[16,256]{1,0:T(8,128)(2,1)}) custom-call(bf16[8,2,5376]{2,1,0:T(2,128)(2,1)S(1)} %get-tuple-element.6.hid_in, bf16[16,256]{1,0:T(8,128)(2,1)S(1)} %get-tuple-element.7.nk_in, bf16[16,256]{1,0:T(8,128)(2,1)S(1)} %get-tuple-element.8.nv_in), custom_call_target="tpu_custom_call" | custom-call | tf_op jit(solution)/shard_map/pallas_call | solution.py:502
